TPU v7x, 32 devices: a whole 2x2x4 slice. The times are simulated.
32 devices in a mesh: fsdp: 4 (over y, x), tensor: 8 (over z, core).
Axes of the slice: x: 2, y: 2, z: 4, core: 2. Of those that a mesh axis runs over, the one named last changes fastest.
Arguments:
- modality: int32 [4096], P('fsdp'), may hold values from 0 to 2, as said below
- out_grad: bfloat16 [4096, 4096], P('fsdp', 'tensor'), may hold values from -6 to 6
- gate_pre: bfloat16 [4096, 11008], P('fsdp', 'tensor'), may hold values from -6 to 6
- up_pre: bfloat16 [4096, 11008], P('fsdp', 'tensor'), may hold values from -6 to 6
- down_weight: bfloat16 [3, 11008, 4096], P(None, 'tensor', 'fsdp'), may hold values from -0.0546875 to 0.0546875
Outputs:
- down_grad: float32 [3, 11008, 4096], P(None, 'tensor', 'fsdp')
- gate_grad: bfloat16 [4096, 11008], P('fsdp', 'tensor')
- up_grad: bfloat16 [4096, 11008], P('fsdp', 'tensor')
Inputs may be any that keep to these rules, and one draw needn't show every extreme that they name: `modality`: the 1024 tokens of every index of fsdp hold each of the three modalities at least once.
All inputs are finite; a program needn't handle non-finite values.
Results may differ from a plain program's by a relative error of at most 0.012.
Values may be sent and summed in bfloat16 or wider, within the bound.
A program may use at most 256 MiB of HBM per device.

v0:
```python
import jax
import jax.numpy as jnp
from jax import lax
from jax.sharding import PartitionSpec as P


def kind_table(kind_ids):
    labels = jnp.arange(3, dtype=jnp.int32)
    return (kind_ids[:, None] == labels[None, :]).astype(jnp.float32)


def shards(modality, out_grad, gate_pre, up_pre, down_weight):
    tok_rows = modality.shape[0]
    groups = lax.axis_size("fsdp")
    local_onehot = kind_table(modality)
    counts = lax.psum(jnp.sum(local_onehot, axis=0), "fsdp")
    factor = tok_rows * groups / (3.0 * counts)
    token_scale = jnp.sum(local_onehot * factor[None, :], axis=1)
    scaled_part = (out_grad.astype(jnp.float32) * token_scale[:, None]).astype(jnp.bfloat16)
    scaled = lax.all_gather(scaled_part, "tensor", axis=1, tiled=True)
    gate_val = gate_pre.astype(jnp.float32)
    up_val = up_pre.astype(jnp.float32)
    sigmoid_g = jax.nn.sigmoid(gate_val)
    active = gate_val * sigmoid_g
    hidden = (active * up_val).astype(jnp.bfloat16)
    hid_cols = hidden.shape[1]
    kind_marks = local_onehot.T.astype(jnp.bfloat16)
    masked_rows = scaled[None, :, :] * kind_marks[:, :, None]
    folded = lax.dot_general(
        masked_rows,
        lax.all_gather(down_weight, "fsdp", axis=2, tiled=True),
        (((0, 2), (0, 2)), ((), ())),
        preferred_element_type=jnp.float32,
    )
    up_grad = (folded * active).astype(jnp.bfloat16)
    slope = sigmoid_g * (1.0 + gate_val * (1.0 - sigmoid_g))
    gate_grad = (folded * up_val * slope).astype(jnp.bfloat16)
    stacked = jnp.broadcast_to(hidden[None, :, :], (3, tok_rows, hid_cols))
    partial_sum = lax.dot_general(
        stacked, masked_rows, (((1,), (1,)), ((0,), (0,))), preferred_element_type=jnp.float32
    )
    down_grad = lax.psum_scatter(
        partial_sum.astype(jnp.bfloat16), "fsdp", scatter_dimension=2, tiled=True
    ).astype(jnp.float32)
    return (down_grad, gate_grad, up_grad)


def solution(mesh):
    placed = (
        P("fsdp"),
        P("fsdp", "tensor"),
        P("fsdp", "tensor"),
        P("fsdp", "tensor"),
        P(None, "tensor", "fsdp"),
    )
    return jax.shard_map(
        shards,
        mesh=mesh,
        in_specs=placed,
        out_specs=(P(None, "tensor", "fsdp"), P("fsdp", "tensor"), P("fsdp", "tensor")),
        check_vma=False,
    )
```

profile of v0, /device:TPU:0, one launch (start us, length us, event | category | flops | bytes accessed | tf_op | source)
XLA Modules:
  0.0 802.1 jit_solution(10436657843060957811)
XLA Ops:
  7.2 0.0 all-gather.3.cloned.1.call-start
  7.2 0.8 convert_reduce_fusion
  8.0 11.4 %psum.7 = f32[3]{0:T(128)S(1)} all-reduce(f32[3]{0:T(128)S(1)} %convert_reduce_fusion), channel_id=1, replica_groups=mesh['fsdp'=4,'tensor'=8] {'fsdp'}, use_global_device_ids=true, to_apply=%region_1.0 | all-reduce | flops 3 | bytes 24 | tf_op jit(solution)/shard_map/psum | solution.py:16
  19.4 0.8 select_reduce_fusion
  20.2 0.0 copy-start
  20.2 2.5 multiply_convert_fusion
  22.7 0.0 all-gather.3.cloned.1.call-update
  22.7 0.0 all-gather.5.cloned.1.call-start
  22.8 0.7 all-gather.5.cloned.1.call-update
  23.5 0.0 reduce-scatter.2.cloned.1.call-start
  23.5 0.0 copy-done
  23.5 80.7 %all-gather.3.cloned.1.call-done = bf16[1024,4096]{1,0:T(8,128)(2,1)} async-done(((bf16[1024,512]{1,0:T(8,128)(2,1)}), bf16[1024,4096]{1,0:T(8,128)(2,1)}) %all-gather.3.cloned.1.call-update) | async-done | bytes 8388624 | tf_op jit(solution)/shard_map/all_gather | solution.py:20
  104.3 300.9 %all-gather.5.cloned.1.call-done = bf16[3,1376,4096]{2,1,0:T(8,128)(2,1)} async-done(((bf16[3,1376,1024]{2,1,0:T(8,128)(2,1)}), bf16[3,1376,4096]{2,1,0:T(8,128)(2,1)}) %all-gather.5.cloned.1.call-update) | async-done | bytes 33816592 | tf_op jit(solution)/shard_map/all_gather | solution.py:31
  405.2 45.4 %fusion.19 = (bf16[1024,1376]{0,1:T(8,128)(2,1)}, bf16[1024,1376]{0,1:T(8,128)(2,1)}, bf16[1024,1376]{0,1:T(8,128)(2,1)S(1)}) fusion(bf16[1024,1376]{0,1:T(8,128)(2,1)} %param.7, bf16[1024,1376]{0,1:T(8,128)(2,1)} %param.8, bf16[3,1376,4096]{2,1,0:T(8,128)(2,1)} %all-gather.5.cloned.1.call-done, bf16[3,1024]{1,0:T(4,128)(2,1)S(1)} %convert_convert_fusion, ...), kind=kOutput, calls=%fused_computation.23 | convolution fusion | flops 34664710144 | bytes 56301568 | tf_op jit(solution)/shard_map/dot_general | solution.py:29
  450.6 1.1 fusion.28
  451.7 41.3 %fusion.4 = bf16[3,1376,4096]{2,1,0:T(8,128)(2,1)} fusion(bf16[3,1024]{1,0:T(4,128)(2,1)S(1)} %convert_convert_fusion, bf16[1024,4096]{1,0:T(8,128)(2,1)} %all-gather.3.cloned.1.call-done, bf16[3,1024,1376]{1,2,0:T(8,128)(2,1)S(1)} %fusion.28), kind=kOutput, calls=%fused_computation.4 | convolution fusion | flops 34657665024 | bytes 50665472 | tf_op jit(solution)/shard_map/dot_general | solution.py:39
  493.0 0.0 reduce-scatter.2.cloned.1.call-update
  493.0 290.8 %reduce-scatter.2.cloned.1.call-done = bf16[3,1376,1024]{2,1,0:T(8,128)(2,1)} async-done(((bf16[3,1376,4096]{2,1,0:T(8,128)(2,1)}), bf16[3,1376,1024]{2,1,0:T(8,128)(2,1)}) %reduce-scatter.2.cloned.1.call-update) | async-done | bytes 8454160 | tf_op jit(solution)/shard_map/reduce_scatter | solution.py:42
  783.8 11.8 %convert_element_type.53 = f32[3,1376,1024]{2,1,0:T(8,128)} convert(bf16[3,1376,1024]{2,1,0:T(8,128)(2,1)} %reduce-scatter.2.cloned.1.call-done) | non-fusion elementwise | flops 4227072 | bytes 25362432 | tf_op jit(solution)/shard_map/convert_element_type | solution.py:44
  (2 shorter events, 0.0 us)
Async XLA Ops:
  7.2 97.1 %all-gather.3.cloned.1.call-start = ((), (), s32[]{:S(2)}) async-start(), calls=%async_computation.1 | async-start | bytes 9437184 | tf_op jit(solution)/shard_map/all_gather | solution.py:20
  20.2 3.3 copy-start
  22.7 382.5 %all-gather.5.cloned.1.call-start = ((), (), s32[]{:S(2)}) async-start(), calls=%async_computation.3 | async-start | bytes 42270720 | tf_op jit(solution)/shard_map/all_gather | solution.py:31
  23.5 760.4 %reduce-scatter.2.cloned.1.call-start = ((), (), s32[]{:S(2)}) async-start(), calls=%async_computation.2 | async-start | bytes 42270720 | tf_op jit(solution)/shard_map/reduce_scatter | solution.py:42
Sparse Core Ops, SparseCore 0:
  22.8 81.3 all-gather.2
  106.1 298.9 all-gather.4
  493.1 290.6 reduce-scatter.1
where the time goes:
time: 802 us
  waiting for transfers between devices  673 us (84%)
  matrix products  86.7 us (11%)
  other arithmetic  15.9 us (2%)
  between operations  13.8 us (2%)
  blocking collectives  11.4 us (1%)
    all_gather x1, waiting for transfers between devices, shards(): lax.all_gather(down_weight, 'fsdp', axis=2, tiled=True)  301 us
    reduce_scatter x1, waiting for transfers between devices, shards(): lax.psum_scatter(partial_sum.astype(jnp.bfloat16), 'fsdp', scatter_dimens...  291 us
    all_gather x1, waiting for transfers between devices, shards(): scaled = lax.all_gather(scaled_part, 'tensor', axis=1, tiled=True)  80.7 us
    dot_general x1, matrix products, shards(): lax.dot_general(masked_rows, lax.all_gather(down_weight, 'fsdp', axis=2,...  45.4 us
    dot_general x1, matrix products, shards(): lax.dot_general(stacked, masked_rows, (((1,), (1,)), ((0,), (0,))), prefe...  41.3 us
  transfers between devices with their start and end apart: 3, of which 3 were waited for; matrix products, arithmetic and copies ran while one was open for 0% of the time, Pallas kernels for 0%

commit v1 on v0

--- a/solution.py
+++ b/solution.py
@@ -17,7 +17,14 @@
     factor = tok_rows * groups / (3.0 * counts)
     token_scale = jnp.sum(local_onehot * factor[None, :], axis=1)
     scaled_part = (out_grad.astype(jnp.float32) * token_scale[:, None]).astype(jnp.bfloat16)
-    scaled = lax.all_gather(scaled_part, "tensor", axis=1, tiled=True)
+    count = lax.axis_size("tensor")
+    forward = [(i, (i + 1) % count) for i in range(count)]
+    pieces = [scaled_part]
+    for far in range(1, count):
+        pieces = [lax.ppermute(pieces[0], "tensor", forward), *pieces]
+    whole = jnp.concatenate(pieces, axis=1)
+    places = (lax.axis_index("tensor") + 1) * pieces[-1].shape[1]
+    scaled = jnp.roll(whole, places, axis=1)
     gate_val = gate_pre.astype(jnp.float32)
     up_val = up_pre.astype(jnp.float32)
     sigmoid_g = jax.nn.sigmoid(gate_val)

time: 802 us -> 713 us (0.89)
  waiting for transfers between devices: 673 us -> 544 us
  local copies, waits for them, and re-layouts: 1.11 us -> 36.9 us
    all_gather x1, waiting for transfers between devices: 301 us -> 141 us  [shards(): lax.all_gather(down_weight, 'fsdp', axis=2, tiled=True)]
    ppermute x0 -> x7, waiting for transfers between devices: none -> 112 us  [shards(): pieces = [lax.ppermute(pieces[0], 'tensor', forward), *pieces]]
    all_gather x1 -> x0, waiting for transfers between devices: 80.7 us -> none  [shards(): scaled = lax.all_gather(scaled_part, 'tensor', axis=1, tiled=True)]
    unnamed x2 -> x28, local copies, waits for them, and re-layouts: 0.01 us -> 26.4 us
  transfers between devices with their start and end apart: 3 -> 9, of which waited for: 3 -> 9; matrix products, arithmetic and copies ran while one was open for 0% -> 5% of each run, Pallas kernels for 0% -> 0%
where the time goes in v1:
time: 713 us; the launch traced here: 712 us
  waiting for transfers between devices  544 us (76%)
  matrix products  86.9 us (12%)
  local copies, waits for them, and re-layouts  36.9 us (5%)
  other arithmetic  18.8 us (3%)
  between operations  14.1 us (2%)
  blocking collectives  11.4 us (2%)
    reduce_scatter x1, waiting for transfers between devices, shards(): lax.psum_scatter(partial_sum.astype(jnp.bfloat16), 'fsdp', scatter_dimens...  291 us
    all_gather x1, waiting for transfers between devices, shards(): lax.all_gather(down_weight, 'fsdp', axis=2, tiled=True)  141 us
    ppermute x7, waiting for transfers between devices, shards(): pieces = [lax.ppermute(pieces[0], 'tensor', forward), *pieces]  112 us
    dot_general x1, matrix products, shards(): lax.dot_general(masked_rows, lax.all_gather(down_weight, 'fsdp', axis=2,...  45.7 us
    dot_general x1, matrix products, shards(): lax.dot_general(stacked, masked_rows, (((1,), (1,)), ((0,), (0,))), prefe...  41.2 us
    unnamed x28, local copies, waits for them, and re-layouts  26.4 us
  transfers between devices with their start and end apart: 9, of which 9 were waited for; matrix products, arithmetic and copies ran while one was open for 5% of the time, Pallas kernels for 0%

profile of v1, /device:TPU:0, one launch (start us, length us, event | category | flops | bytes accessed | tf_op | source)
XLA Modules:
  0.0 712.4 jit_solution(9087198287868958616)
XLA Ops:
  7.2 0.0 copy-start
  7.2 0.0 all-gather.2.cloned.1.call-start
  7.2 0.7 all-gather.2.cloned.1.call-update
  7.9 0.0 reduce-scatter.2.cloned.1.call-start
  8.0 0.8 convert_reduce_fusion
  8.8 11.4 %psum.7 = f32[3]{0:T(128)S(1)} all-reduce(f32[3]{0:T(128)S(1)} %convert_reduce_fusion), channel_id=1, replica_groups=mesh['fsdp'=4,'tensor'=8] {'fsdp'}, use_global_device_ids=true, to_apply=%region_1.0 | all-reduce | flops 3 | bytes 24 | tf_op jit(solution)/shard_map/psum | solution.py:16
  20.2 0.8 select_reduce_fusion
  20.9 2.1 multiply_convert_fusion
  23.0 0.1 collective-permute-start
  23.1 16.0 %collective-permute-done = bf16[1024,512]{1,0:T(8,128)(2,1)S(1)} collective-permute-done((bf16[1024,512]{1,0:T(8,128)(2,1)S(1)}, bf16[1024,512]{1,0:T(8,128)(2,1)S(1)}, u32[]{:S(2)}, u32[]{:S(2)}) %collective-permute-start) | collective-permute-done | bytes 1048608 | tf_op jit(solution)/shard_map/ppermute | solution.py:24
  39.1 0.0 collective-permute-start.1
  39.1 16.0 %collective-permute-done.1 = bf16[1024,512]{1,0:T(8,128)(2,1)S(1)} collective-permute-done((bf16[1024,512]{1,0:T(8,128)(2,1)S(1)}, bf16[1024,512]{1,0:T(8,128)(2,1)S(1)}, u32[]{:S(2)}, u32[]{:S(2)}) %collective-permute-start.1) | collective-permute-done | bytes 1048608 | tf_op jit(solution)/shard_map/ppermute | solution.py:24
  55.1 16.0 %collective-permute-done.2 = bf16[1024,512]{1,0:T(8,128)(2,1)S(1)} collective-permute-done((bf16[1024,512]{1,0:T(8,128)(2,1)S(1)}, bf16[1024,512]{1,0:T(8,128)(2,1)S(1)}, u32[]{:S(2)}, u32[]{:S(2)}) %collective-permute-start.2) | collective-permute-done | bytes 1048608 | tf_op jit(solution)/shard_map/ppermute | solution.py:24
  71.1 1.0 copy-done.1
  72.1 16.0 %collective-permute-done.3 = bf16[1024,512]{1,0:T(8,128)(2,1)S(1)} collective-permute-done((bf16[1024,512]{1,0:T(8,128)(2,1)S(1)}, bf16[1024,512]{1,0:T(8,128)(2,1)S(1)}, u32[]{:S(2)}, u32[]{:S(2)}) %collective-permute-start.3) | collective-permute-done | bytes 1048608 | tf_op jit(solution)/shard_map/ppermute | solution.py:24
  88.2 1.0 copy-done.3
  89.1 0.0 collective-permute-start.4
  89.1 16.0 %collective-permute-done.4 = bf16[1024,512]{1,0:T(8,128)(2,1)S(1)} collective-permute-done((bf16[1024,512]{1,0:T(8,128)(2,1)S(1)}, bf16[1024,512]{1,0:T(8,128)(2,1)S(1)}, u32[]{:S(2)}, u32[]{:S(2)}) %collective-permute-start.4) | collective-permute-done | bytes 1048608 | tf_op jit(solution)/shard_map/ppermute | solution.py:24
  105.2 1.0 copy-done.5
  106.1 0.0 collective-permute-start.5
  106.1 16.1 %collective-permute-done.5 = bf16[1024,512]{1,0:T(8,128)(2,1)} collective-permute-done((bf16[1024,512]{1,0:T(8,128)(2,1)S(1)}, bf16[1024,512]{1,0:T(8,128)(2,1)}, u32[]{:S(2)}, u32[]{:S(2)}) %collective-permute-start.5) | collective-permute-done | bytes 1048608 | tf_op jit(solution)/shard_map/ppermute | solution.py:24
  122.2 0.0 collective-permute-start.6
  122.3 0.8 convert_convert_fusion
  123.1 15.5 %collective-permute-done.6 = bf16[1024,512]{1,0:T(8,128)(2,1)} collective-permute-done((bf16[1024,512]{1,0:T(8,128)(2,1)}, bf16[1024,512]{1,0:T(8,128)(2,1)}, u32[]{:S(2)}, u32[]{:S(2)}) %collective-permute-start.6) | collective-permute-done | bytes 1048608 | tf_op jit(solution)/shard_map/ppermute | solution.py:24
  138.6 2.6 constant_dynamic-update-slice_fusion.15
  141.2 2.3 constant_dynamic-update-slice_fusion.14
  143.4 2.3 constant_dynamic-update-slice_fusion.13
  145.7 2.3 constant_dynamic-update-slice_fusion.12
  147.9 2.3 constant_dynamic-update-slice_fusion.11
  150.2 1.0 constant_dynamic-update-slice_fusion.10
  151.2 1.0 constant_dynamic-update-slice_fusion.9
  152.3 1.3 constant_dynamic-update-slice_fusion.8
  153.5 2.3 constant_dynamic-update-slice_fusion.7
  155.8 2.3 constant_dynamic-update-slice_fusion.6
  158.1 1.0 constant_dynamic-update-slice_fusion.5
  159.1 1.0 constant_dynamic-update-slice_fusion.4
  160.2 1.0 constant_dynamic-update-slice_fusion.3
  161.2 1.0 constant_dynamic-update-slice_fusion.2
  162.2 1.0 constant_dynamic-update-slice_fusion.1
  163.3 1.3 constant_dynamic-update-slice_fusion
  164.5 7.7 %constant_dynamic-slice_fusion = bf16[1024,4096]{1,0:T(8,128)(2,1)} fusion(bf16[1024,8192]{1,0:T(8,128)(2,1)} %constant_dynamic-update-slice_fusion, s32[]{:T(128)S(6)} %select_n.14), kind=kLoop, calls=%fused_computation.48 | loop fusion | bytes 16777220 | tf_op jit(solution)/shard_map/jit(_roll_dynamic)/dynamic_slice | solution.py:27
  172.2 140.9 %all-gather.2.cloned.1.call-done = bf16[3,1376,4096]{2,1,0:T(8,128)(2,1)} async-done(((bf16[3,1376,1024]{2,1,0:T(8,128)(2,1)}), bf16[3,1376,4096]{2,1,0:T(8,128)(2,1)}) %all-gather.2.cloned.1.call-update) | async-done | bytes 33816592 | tf_op jit(solution)/shard_map/all_gather | solution.py:38
  313.1 45.7 %fusion.19 = (bf16[1024,1376]{0,1:T(8,128)(2,1)}, bf16[1024,1376]{0,1:T(8,128)(2,1)}, bf16[1024,1376]{0,1:T(8,128)(2,1)}) fusion(bf16[1024,1376]{0,1:T(8,128)(2,1)} %param.7, bf16[1024,1376]{0,1:T(8,128)(2,1)} %param.8, bf16[3,1376,4096]{2,1,0:T(8,128)(2,1)} %all-gather.2.cloned.1.call-done, bf16[3,1024]{1,0:T(4,128)(2,1)S(1)} %convert_convert_fusion, ...), kind=kOutput, calls=%fused_computation.23 | convolution fusion | flops 34664710144 | bytes 56301568 | tf_op jit(solution)/shard_map/dot_general | solution.py:36
  358.8 2.9 fusion.28
  361.7 41.2 %fusion.4 = bf16[3,1376,4096]{2,1,0:T(8,128)(2,1)} fusion(bf16[3,1024]{1,0:T(4,128)(2,1)S(1)} %convert_convert_fusion, bf16[1024,4096]{1,0:T(8,128)(2,1)} %constant_dynamic-slice_fusion, bf16[3,1024,1376]{1,2,0:T(8,128)(2,1)S(1)} %fusion.28), kind=kOutput, calls=%fused_computation.4 | convolution fusion | flops 34657665024 | bytes 50665472 | tf_op jit(solution)/shard_map/dot_general | solution.py:46
  402.9 0.0 reduce-scatter.2.cloned.1.call-update
  402.9 290.8 %reduce-scatter.2.cloned.1.call-done = bf16[3,1376,1024]{2,1,0:T(8,128)(2,1)} async-done(((bf16[3,1376,4096]{2,1,0:T(8,128)(2,1)}), bf16[3,1376,1024]{2,1,0:T(8,128)(2,1)}) %reduce-scatter.2.cloned.1.call-update) | async-done | bytes 8454160 | tf_op jit(solution)/shard_map/reduce_scatter | solution.py:49
  693.8 11.8 %convert_element_type.53 = f32[3,1376,1024]{2,1,0:T(8,128)} convert(bf16[3,1376,1024]{2,1,0:T(8,128)(2,1)} %reduce-scatter.2.cloned.1.call-done) | non-fusion elementwise | flops 4227072 | bytes 25362432 | tf_op jit(solution)/shard_map/convert_element_type | solution.py:51
  (13 shorter events, 0.0 us)
Async XLA Ops:
  7.2 145.1 %copy-start = (bf16[1024,512]{1,0:T(8,128)(2,1)S(1)}, bf16[1024,512]{1,0:T(8,128)(2,1)}, u32[]{:S(2)}) copy-start(bf16[1024,512]{1,0:T(8,128)(2,1)} %param.6) | copy-start | bytes 3145732
  7.2 305.9 %all-gather.2.cloned.1.call-start = ((), (), s32[]{:S(2)}) async-start(), calls=%async_computation.2 | async-start | bytes 42270720 | tf_op jit(solution)/shard_map/all_gather | solution.py:38
  7.9 685.9 %reduce-scatter.2.cloned.1.call-start = ((), (), s32[]{:S(2)}) async-start(), calls=%async_computation.1 | async-start | bytes 42270720 | tf_op jit(solution)/shard_map/reduce_scatter | solution.py:49
  23.0 16.1 %collective-permute-start = (bf16[1024,512]{1,0:T(8,128)(2,1)S(1)}, bf16[1024,512]{1,0:T(8,128)(2,1)S(1)}, u32[]{:S(2)}, u32[]{:S(2)}) collective-permute-start(bf16[1024,512]{1,0:T(8,128)(2,1)S(1)} %multiply_convert_fusion), channel_id=1, source_target_pairs={{0,1},{1,2},{2,3},{3,4},{4,5},{5,6},{6,7},{7,0},{8,9},{9,10},{10,1... | collective-permute-start | bytes 3145736 | tf_op jit(solution)/shard_map/ppermute | solution.py:24
  39.1 16.0 %collective-permute-start.1 = (bf16[1024,512]{1,0:T(8,128)(2,1)S(1)}, bf16[1024,512]{1,0:T(8,128)(2,1)S(1)}, u32[]{:S(2)}, u32[]{:S(2)}) collective-permute-start(bf16[1024,512]{1,0:T(8,128)(2,1)S(1)} %collective-permute-done), channel_id=1, source_target_pairs={{0,1},{1,2},{2,3},{3,4},{4,5},{5,6},{6,7},{7,0},{8,9},{9,10},{10,1... | collective-permute-start | bytes 3145736 | tf_op jit(solution)/shard_map/ppermute | solution.py:24
  55.1 16.0 %collective-permute-start.2 = (bf16[1024,512]{1,0:T(8,128)(2,1)S(1)}, bf16[1024,512]{1,0:T(8,128)(2,1)S(1)}, u32[]{:S(2)}, u32[]{:S(2)}) collective-permute-start(bf16[1024,512]{1,0:T(8,128)(2,1)S(1)} %collective-permute-done.1), channel_id=1, source_target_pairs={{0,1},{1,2},{2,3},{3,4},{4,5},{5,6},{6,7},{7,0},{8,9},{9,10},{10,1... | collective-permute-start | bytes 3145736 | tf_op jit(solution)/shard_map/ppermute | solution.py:24
  71.1 1.0 copy-start.1
  72.1 16.0 %collective-permute-start.3 = (bf16[1024,512]{1,0:T(8,128)(2,1)S(1)}, bf16[1024,512]{1,0:T(8,128)(2,1)S(1)}, u32[]{:S(2)}, u32[]{:S(2)}) collective-permute-start(bf16[1024,512]{1,0:T(8,128)(2,1)S(1)} %collective-permute-done.2), channel_id=1, source_target_pairs={{0,1},{1,2},{2,3},{3,4},{4,5},{5,6},{6,7},{7,0},{8,9},{9,10},{10,1... | collective-permute-start | bytes 3145736 | tf_op jit(solution)/shard_map/ppermute | solution.py:24
  88.2 1.0 copy-start.3
  89.1 16.0 %collective-permute-start.4 = (bf16[1024,512]{1,0:T(8,128)(2,1)S(1)}, bf16[1024,512]{1,0:T(8,128)(2,1)S(1)}, u32[]{:S(2)}, u32[]{:S(2)}) collective-permute-start(bf16[1024,512]{1,0:T(8,128)(2,1)S(1)} %collective-permute-done.3), channel_id=1, source_target_pairs={{0,1},{1,2},{2,3},{3,4},{4,5},{5,6},{6,7},{7,0},{8,9},{9,10},{10,1... | collective-permute-start | bytes 3145736 | tf_op jit(solution)/shard_map/ppermute | solution.py:24
  105.2 1.0 copy-start.5
  106.1 16.1 %collective-permute-start.5 = (bf16[1024,512]{1,0:T(8,128)(2,1)S(1)}, bf16[1024,512]{1,0:T(8,128)(2,1)}, u32[]{:S(2)}, u32[]{:S(2)}) collective-permute-start(bf16[1024,512]{1,0:T(8,128)(2,1)S(1)} %collective-permute-done.4), channel_id=1, source_target_pairs={{0,1},{1,2},{2,3},{3,4},{4,5},{5,6},{6,7},{7,0},{8,9},{9,10},{10,1... | collective-permute-start | bytes 3145736 | tf_op jit(solution)/shard_map/ppermute | solution.py:24
  122.2 16.3 %collective-permute-start.6 = (bf16[1024,512]{1,0:T(8,128)(2,1)}, bf16[1024,512]{1,0:T(8,128)(2,1)}, u32[]{:S(2)}, u32[]{:S(2)}) collective-permute-start(bf16[1024,512]{1,0:T(8,128)(2,1)} %collective-permute-done.5), channel_id=1, source_target_pairs={{0,1},{1,2},{2,3},{3,4},{4,5},{5,6},{6,7},{7,0},{8,9},{9,10},{10,1... | collective-permute-start | bytes 3145736 | tf_op jit(solution)/shard_map/ppermute | solution.py:24
  122.3 35.8 %copy-start.6 = (bf16[1024,512]{1,0:T(8,128)(2,1)S(1)}, bf16[1024,512]{1,0:T(8,128)(2,1)}, u32[]{:S(2)}) copy-start(bf16[1024,512]{1,0:T(8,128)(2,1)} %copy-done.5) | copy-start | bytes 3145732
  122.3 36.9 %copy-start.4 = (bf16[1024,512]{1,0:T(8,128)(2,1)S(1)}, bf16[1024,512]{1,0:T(8,128)(2,1)}, u32[]{:S(2)}) copy-start(bf16[1024,512]{1,0:T(8,128)(2,1)} %copy-done.3) | copy-start | bytes 3145732
  122.3 37.9 %copy-start.2 = (bf16[1024,512]{1,0:T(8,128)(2,1)S(1)}, bf16[1024,512]{1,0:T(8,128)(2,1)}, u32[]{:S(2)}) copy-start(bf16[1024,512]{1,0:T(8,128)(2,1)} %copy-done.1) | copy-start | bytes 3145732
Sparse Core Ops, SparseCore 0:
  9.9 303.2 all-gather.1
  403.0 290.6 reduce-scatter.1
